TPU v7x, 8 devices: a whole 2x2x1 slice. The times are simulated.
8 devices in a mesh: member: 1 (over z), lon: 2 (over y), lat: 4 (over x, core).
Axes of the slice: x: 2, y: 2, z: 1, core: 2. Of those that a mesh axis runs over, the one named last changes fastest.
Arguments:
- grid_field: float32 [6, 384, 180, 360], P('member', None, 'lat', 'lon')
- mix_weight: bfloat16 [180, 384, 384, 2], replicated
Outputs:
- output: float32 [6, 384, 180, 360], P('member', None, 'lat', 'lon')
All inputs are finite; a program needn't handle non-finite values.
Results may differ from a plain program's by a relative error of at most 0.00404289.
Values are sent between devices in bfloat16 or wider.
A program may use at most 1 GiB of HBM per device.

v0:
```python
import math
import jax
import jax.numpy as jnp
from jax import lax
from jax.sharding import PartitionSpec as P, NamedSharding


def legendre_table(m_vals, colatitude, n_deg):
    cos_t = jnp.cos(colatitude)[None, :]
    m_int = m_vals[:, None]
    m_col = m_int.astype(jnp.float32)
    deg_all = jnp.arange(1, n_deg + 1).astype(jnp.float32)
    log_steps = 0.5 * jnp.log((2.0 * deg_all + 1.0) / (2.0 * deg_all))
    cum_log = jnp.concatenate([jnp.zeros((1,), jnp.float32), jnp.cumsum(log_steps)])
    log_diag = 0.5 * math.log(0.5) + cum_log[m_vals][:, None] + m_col * jnp.log(jnp.sin(colatitude))[None, :]

    def degree_step(carry, degree):
        prev_one, prev_two, log_scale = carry
        deg_f = degree.astype(jnp.float32)
        at_start = m_int == degree
        is_above = m_int < degree
        coef_a = jnp.sqrt((4.0 * deg_f * deg_f - 1.0) / jnp.maximum(deg_f * deg_f - m_col * m_col, 1.0))
        coef_b = jnp.sqrt(jnp.maximum((deg_f - 1.0) ** 2 - m_col * m_col, 0.0) / jnp.maximum(4.0 * (deg_f - 1.0) ** 2 - 1.0, 1.0))
        rec_value = coef_a * (cos_t * prev_one - coef_b * prev_two)
        renorm = jnp.maximum(jnp.abs(rec_value), 1.0)
        next_one = jnp.where(at_start, 1.0, jnp.where(is_above, rec_value / renorm, 0.0))
        next_two = jnp.where(is_above, prev_one / renorm, 0.0)
        next_scale = jnp.where(at_start, log_diag, jnp.where(is_above, log_scale + jnp.log(renorm), 0.0))
        out_value = jnp.where(at_start | is_above, next_one * jnp.exp(next_scale), 0.0)
        return (next_one, next_two, next_scale), out_value

    zero_state = jnp.zeros((m_vals.shape[0], colatitude.shape[0]), jnp.float32)
    return lax.scan(degree_step, (zero_state, zero_state, zero_state), jnp.arange(n_deg))[1]


def fejer_weights(colatitude, n_lat):
    harmonic = jnp.arange(1, n_lat // 2 + 1).astype(jnp.float32)
    series = jnp.cos(2.0 * colatitude[:, None] * harmonic[None, :]) / (4.0 * harmonic * harmonic - 1.0)
    return (2.0 / n_lat) * (1.0 - 2.0 * jnp.sum(series, axis=1))


def dft_tables(n_lon, n_deg):
    lon_index = jnp.arange(n_lon)
    deg_index = jnp.arange(n_deg)
    fwd_angle = ((lon_index[:, None] * deg_index[None, :]) % n_lon).astype(jnp.float32) * (2.0 * math.pi / n_lon)
    fwd_table = jnp.concatenate([jnp.cos(fwd_angle), -jnp.sin(fwd_angle)], axis=1).astype(jnp.bfloat16)
    inv_angle = ((deg_index[:, None] * lon_index[None, :]) % n_lon).astype(jnp.float32) * (2.0 * math.pi / n_lon)
    weight_m = jnp.where(deg_index == 0, 1.0, 2.0)[:, None]
    inv_table = jnp.concatenate([weight_m * jnp.cos(inv_angle), -weight_m * jnp.sin(inv_angle)], axis=0).astype(jnp.bfloat16)
    return fwd_table, inv_table


def mixing_block(mix_weight):
    flipped = jnp.stack([-mix_weight[..., 1], mix_weight[..., 0]], axis=-1)
    return jnp.stack([mix_weight, flipped], axis=2)


def solution(mesh):
    lat_devs = mesh.shape['lat']
    lon_devs = mesh.shape['lon']

    def local_layer(grid_field, mix_weight):
        batch_local, channels, row_count, col_count = grid_field.shape
        n_lat = row_count * lat_devs
        n_lon = col_count * lon_devs
        n_deg = mix_weight.shape[0]
        m_per = n_deg // lat_devs
        l_per = n_deg // lon_devs
        chan_local = channels // lon_devs
        lat_rank = lax.axis_index('lat')
        lon_rank = lax.axis_index('lon')
        fwd_table, inv_table = dft_tables(n_lon, n_deg)
        colatitude = (jnp.arange(n_lat).astype(jnp.float32) + 0.5) * (math.pi / n_lat)
        leg_table = legendre_table(lat_rank * m_per + jnp.arange(m_per), colatitude, n_deg)
        leg_fwd = (leg_table * (fejer_weights(colatitude, n_lat) / n_lon)).astype(jnp.bfloat16)
        leg_inv = leg_table.astype(jnp.bfloat16)
        w_block = mixing_block(lax.dynamic_slice_in_dim(mix_weight, lon_rank * l_per, l_per, axis=0))

        grid_bf = lax.all_to_all(grid_field.astype(jnp.bfloat16), 'lon', 1, 3, tiled=True)
        fourier = jnp.dot(grid_bf.reshape(-1, n_lon), fwd_table, preferred_element_type=jnp.float32)
        fourier = fourier.astype(jnp.bfloat16).reshape(batch_local, chan_local, row_count, 2, n_deg)
        fourier = lax.all_to_all(fourier, 'lat', 4, 2, tiled=True)
        spec_coef = jnp.einsum('bckrm,lmk->bclrm', fourier, leg_fwd, preferred_element_type=jnp.float32).astype(jnp.bfloat16)
        spec_coef = lax.all_to_all(spec_coef, 'lon', 2, 1, tiled=True)
        mixed_coef = jnp.einsum('bilsm,lisor->bolrm', spec_coef, w_block, preferred_element_type=jnp.float32).astype(jnp.bfloat16)
        mixed_coef = lax.all_to_all(mixed_coef, 'lon', 1, 2, tiled=True)
        spec_grid = jnp.einsum('bclrm,lmk->bckrm', mixed_coef, leg_inv, preferred_element_type=jnp.float32).astype(jnp.bfloat16)
        spec_grid = lax.all_to_all(spec_grid, 'lat', 2, 4, tiled=True)
        grid_out = jnp.dot(spec_grid.reshape(-1, 2 * n_deg), inv_table, preferred_element_type=jnp.float32)
        grid_out = grid_out.astype(jnp.bfloat16).reshape(batch_local, chan_local, row_count, n_lon)
        grid_out = lax.all_to_all(grid_out, 'lon', 3, 1, tiled=True)
        return grid_field + jax.nn.gelu(grid_out.astype(jnp.float32), approximate=False)

    field_spec = P('member', None, 'lat', 'lon')
    return jax.shard_map(local_layer, mesh=mesh, in_specs=(field_spec, P()), out_specs=field_spec, check_vma=False)
```

profile of v0, /device:TPU:0, one launch (start us, length us, event | category | flops | bytes accessed | tf_op | source)
XLA Modules:
  0.0 6789.6 jit_solution(17051360423702799889)
XLA Ops:
  0.0 36.6 convert_element_type.120
  36.6 74.6 %copy.151 = bf16[6,384,45,180]{3,2,0,1:T(8,128)(2,1)} copy(bf16[6,384,45,180]{1,3,2,0:T(8,128)(2,1)} %convert_element_type.120) | data formatting | bytes 74649600 | tf_op jit(solution)/shard_map/convert_element_type | solution.py:79
  111.2 21.2 all-to-all-start
  135.1 1.6 negate_convert_fusion
  137.3 605.8 %all-to-all-done = bf16[6,384,45,180]{3,2,0,1:T(8,128)(2,1)} async-done(((bf16[6,384,45,180]{3,2,0,1:T(8,128)(2,1)}), bf16[6,384,45,180]{3,2,0,1:T(8,128)(2,1)}, u32[]{:S(2)}, u32[]{:S(2)}) %all-to-all-start) | async-done | bytes 37324832 | tf_op jit(solution)/shard_map/all_to_all | solution.py:79
  743.1 89.5 %copy.210 = bf16[6,2,192,45,180]{4,1,3,2,0:T(2,128)(2,1)} copy(bf16[6,2,192,45,180]{4,3,0,2,1:T(8,128)(2,1)} %bitcast.9) | data formatting | bytes 74649600 | tf_op jit(solution)/shard_map/all_to_all | solution.py:79
  832.6 104.8 %reshape.186 = bf16[51840,360]{1,0:T(8,128)(2,1)} reshape(bf16[6,192,45,2,180]{4,3,2,1,0:T(2,128)(2,1)} %bitcast.118) | data formatting | bytes 74649600 | tf_op jit(solution)/shard_map/reshape | solution.py:80
  937.4 34.2 fusion.25
  971.7 306.3 %reshape.205 = bf16[6,192,45,2,180]{2,1,0,4,3:T(8,128)(2,1)} reshape(bf16[51840,360]{0,1:T(8,128)(2,1)} %fusion.25) | data formatting | bytes 74649600 | tf_op jit(solution)/shard_map/reshape | solution.py:81
  1278.0 158.2 %copy.154 = bf16[6,192,45,2,180]{1,3,2,0,4:T(2,128)(2,1)} copy(bf16[6,192,45,2,180]{2,1,0,4,3:T(8,128)(2,1)} %reshape.205) | data formatting | bytes 74649600 | tf_op jit(solution)/shard_map/reshape | solution.py:81
  1436.2 12.1 all-to-all-start.1
  1448.4 538.3 %while.22 = (s32[]{:T(128)}, f32[45,180]{1,0:T(8,128)S(1)}, f32[45,180]{1,0:T(8,128)S(1)}, f32[45,180]{1,0:T(8,128)S(1)}, f32[180,45,180]{2,1,0:T(8,128)}, /*ind...) while((s32[]{:T(128)}, f32[45,180]{1,0:T(8,128)S(1)}, ...), condition=%wide.region_3.4_spmd.clone.clone.clone, body=%wide.region_2.3_spmd.clone.clone.clone.sunk | while | flops 236038 | bytes 378107 | solution.py:33
  1987.2 11.2 convert_bitcast_fusion.2
  1998.4 45.8 copy.156
  2044.2 51.8 convert_bitcast_fusion.1
  2096.0 69.7 %copy.159 = bf16[6,192,180,2,45]{1,3,4,0,2:T(2,128)(2,1)} copy(bf16[6,192,180,2,45]{1,2,3,0,4:T(8,128)(2,1)} %convert_bitcast_fusion.1) | data formatting | bytes 74649600 | tf_op jit(solution)/shard_map/convert_element_type | solution.py:83
  2165.7 18.6 all-to-all-start.2
  2184.3 43.6 constant_dynamic-slice_fusion
  2227.9 35.4 copy.211
  2263.3 34.9 slice_negate_fusion
  2298.2 35.6 maximum_bitcast_fusion.2
  2333.9 386.7 %all-to-all-done.2 = bf16[6,192,180,2,45]{1,3,4,0,2:T(2,128)(2,1)} async-done(((bf16[6,192,180,2,45]{1,3,4,0,2:T(2,128)(2,1)}), bf16[6,192,180,2,45]{1,3,4,0,2:T(2,128)(2,1)}, u32[]{:S(2)}, u32[]{:S(2)}) %all-to-all-start.2) | async-done | bytes 37324832 | tf_op jit(solution)/shard_map/all_to_all | solution.py:84
  2720.6 72.6 %copy.189 = bf16[6,2,192,90,2,45]{2,1,5,4,0,3:T(2,128)(2,1)} copy(bf16[6,2,192,90,2,45]{2,4,5,0,3,1:T(2,128)(2,1)} %bitcast.19) | data formatting | bytes 74649600 | tf_op jit(solution)/shard_map/all_to_all | solution.py:84
  2793.2 99.3 %reshape.202 = bf16[6,384,90,2,45,1]{1,4,3,0,2,5:T(8,128)(2,1)} reshape(bf16[6,2,192,90,2,45]{2,1,5,4,0,3:T(2,128)(2,1)} %copy.189) | data formatting | bytes 74649600 | tf_op jit(solution)/shard_map/all_to_all | solution.py:84
  2892.4 63.2 fusion.30
  2955.6 97.1 %copy.163 = bf16[6,384,90,2,45]{2,3,4,0,1:T(2,128)(2,1)} copy(bf16[6,384,90,2,45]{1,4,0,3,2:T(8,128)(2,1)} %fusion.30) | data formatting | bytes 74649600 | tf_op jit(solution)/shard_map/convert_element_type | solution.py:85
  3052.7 619.9 %all_to_all.93 = bf16[6,384,90,2,45]{2,3,4,0,1:T(2,128)(2,1)} all-to-all(bf16[6,384,90,2,45]{2,3,4,0,1:T(2,128)(2,1)} %copy.163), channel_id=1, replica_groups=mesh['member'=1,'lon'=2,'lat'=4] {'lon'}, dimensions={1} | all-to-all | bytes 74649600 | tf_op jit(solution)/shard_map/all_to_all | solution.py:86
  3672.7 174.3 %copy.165 = bf16[6,192,2,90,2,45]{1,4,5,3,2,0:T(2,128)(2,1)} copy(bf16[6,192,2,90,2,45]{3,4,5,0,1,2:T(2,128)(2,1)} %bitcast.117) | data formatting | bytes 74649600 | tf_op jit(solution)/shard_map/all_to_all | solution.py:86
  3847.0 53.1 convert_bitcast_fusion
  3900.0 69.7 %copy.168 = bf16[6,192,180,2,45]{1,3,4,0,2:T(2,128)(2,1)} copy(bf16[6,192,180,2,45]{1,2,3,0,4:T(8,128)(2,1)} %convert_bitcast_fusion) | data formatting | bytes 74649600 | tf_op jit(solution)/shard_map/convert_element_type | solution.py:87
  3969.7 12.0 all-to-all-start.4
  3983.0 534.9 %all-to-all-done.4 = bf16[6,192,180,2,45]{1,3,4,0,2:T(2,128)(2,1)} async-done(((bf16[6,192,180,2,45]{1,3,4,0,2:T(2,128)(2,1)}), bf16[6,192,180,2,45]{1,3,4,0,2:T(2,128)(2,1)}, u32[]{:S(2)}, u32[]{:S(2)}) %all-to-all-start.4) | async-done | bytes 37324832 | tf_op jit(solution)/shard_map/all_to_all | solution.py:88
  4517.9 156.9 %copy.170 = bf16[6,192,45,2,4,45]{2,1,0,5,4,3:T(8,128)(2,1)} copy(bf16[6,192,45,2,4,45]{1,3,5,0,2,4:T(2,128)(2,1)} %bitcast.31) | data formatting | bytes 74649600 | tf_op jit(solution)/shard_map/all_to_all | solution.py:88
  4674.8 158.1 %reshape.188 = bf16[51840,360]{0,1:T(8,128)(2,1)} reshape(bf16[6,192,45,2,4,45]{2,1,0,5,4,3:T(8,128)(2,1)} %copy.170) | data formatting | bytes 74649600 | tf_op jit(solution)/shard_map/reshape | solution.py:89
  4832.9 31.9 convolution_convert_fusion
  4864.8 51.0 copy.171
  4915.8 55.5 reshape.189
  4971.2 74.6 %copy.172 = bf16[6,192,45,360]{1,2,0,3:T(8,128)(2,1)} copy(bf16[6,192,45,360]{3,2,1,0:T(8,128)(2,1)} %reshape.189) | data formatting | bytes 74649600 | tf_op jit(solution)/shard_map/reshape | solution.py:90
  5045.8 620.0 %all_to_all.94 = bf16[6,192,45,360]{1,2,0,3:T(8,128)(2,1)} all-to-all(bf16[6,192,45,360]{1,2,0,3:T(8,128)(2,1)} %copy.172), channel_id=1, replica_groups=mesh['member'=1,'lon'=2,'lat'=4] {'lon'}, dimensions={3} | all-to-all | bytes 74649600 | tf_op jit(solution)/shard_map/all_to_all | solution.py:91
  5665.7 66.9 copy.173
  5732.6 61.9 fusion.15
  5794.6 125.8 %reshape.191 = f32[6,192,45,2,180]{4,3,1,2,0:T(2,128)} reshape(f32[6,192,45,360]{3,1,2,0:T(8,128)} %get-tuple-element.299) | data formatting | bytes 149299200 | tf_op jit(solution)/shard_map/mul | solution.py:92
  5920.4 185.8 %copy.175 = f32[6,2,192,45,180]{2,1,4,3,0:T(2,128)} copy(f32[6,2,192,45,180]{4,1,2,3,0:T(2,128)} %bitcast.33) | data formatting | bytes 149299200 | tf_op jit(solution)/shard_map/mul | solution.py:92
  6106.1 104.4 %mul.359 = f32[6,384,45,180]{1,3,2,0:T(8,128)} reshape(f32[6,2,192,45,180]{2,1,4,3,0:T(2,128)} %copy.175) | data formatting | bytes 149299200 | tf_op jit(solution)/shard_map/mul | solution.py:92
  6210.5 125.8 %mul.353 = f32[6,192,45,2,180]{4,3,1,2,0:T(2,128)} reshape(f32[6,192,45,360]{3,1,2,0:T(8,128)} %get-tuple-element.300) | data formatting | bytes 149299200 | tf_op jit(solution)/shard_map/mul | solution.py:92
  6336.3 185.8 %copy.174 = f32[6,2,192,45,180]{2,1,4,3,0:T(2,128)} copy(f32[6,2,192,45,180]{4,1,2,3,0:T(2,128)} %bitcast.32) | data formatting | bytes 149299200 | tf_op jit(solution)/shard_map/mul | solution.py:92
  6522.1 104.4 %mul.355 = f32[6,384,45,180]{1,3,2,0:T(8,128)} reshape(f32[6,2,192,45,180]{2,1,4,3,0:T(2,128)} %copy.174) | data formatting | bytes 149299200 | tf_op jit(solution)/shard_map/mul | solution.py:92
  6626.4 162.8 %fusion.18 = f32[6,384,45,180]{1,3,2,0:T(8,128)} fusion(f32[6,384,45,180]{1,3,2,0:T(8,128)} %param.4, f32[6,384,45,180]{1,3,2,0:T(8,128)} %mul.355, f32[6,384,45,180]{1,3,2,0:T(8,128)} %mul.359), kind=kLoop, calls=%fused_computation.33 | loop fusion | flops 1157068800 | bytes 298598400 | tf_op jit(solution)/shard_map/add | solution.py:92
  (1300 shorter events, 412.8 us)
Async XLA Ops:
  111.2 631.9 %all-to-all-start = ((bf16[6,384,45,180]{3,2,0,1:T(8,128)(2,1)}), bf16[6,384,45,180]{3,2,0,1:T(8,128)(2,1)}, u32[]{:S(2)}, u32[]{:S(2)}) async-start(bf16[6,384,45,180]{3,2,0,1:T(8,128)(2,1)} %copy.151), calls=%async_computation | async-start | bytes 113246208 | tf_op jit(solution)/shard_map/all_to_all | solution.py:79
  1436.1 12.2 copy-start
  1436.1 12.2 copy-start.1
  1436.1 12.2 copy-start.2
  1436.1 12.2 copy-start.3
  1436.1 12.2 copy-start.4
  1436.1 12.2 copy-start.5
  1436.2 562.2 %all-to-all-start.1 = ((bf16[6,192,45,2,180]{1,3,2,0,4:T(2,128)(2,1)}), bf16[6,192,45,2,180]{1,3,2,0,4:T(2,128)(2,1)}, u32[]{:S(2)}, u32[]{:S(2)}) async-start(bf16[6,192,45,2,180]{1,3,2,0,4:T(2,128)(2,1)} %copy.154), calls=%async_computation.1 | async-start | bytes 99532800 | tf_op jit(solution)/shard_map/all_to_all | solution.py:82
  2165.7 554.9 %all-to-all-start.2 = ((bf16[6,192,180,2,45]{1,3,4,0,2:T(2,128)(2,1)}), bf16[6,192,180,2,45]{1,3,4,0,2:T(2,128)(2,1)}, u32[]{:S(2)}, u32[]{:S(2)}) async-start(bf16[6,192,180,2,45]{1,3,4,0,2:T(2,128)(2,1)} %copy.159), calls=%async_computation.2 | async-start | bytes 99532800 | tf_op jit(solution)/shard_map/all_to_all | solution.py:84
  3969.7 548.2 %all-to-all-start.4 = ((bf16[6,192,180,2,45]{1,3,4,0,2:T(2,128)(2,1)}), bf16[6,192,180,2,45]{1,3,4,0,2:T(2,128)(2,1)}, u32[]{:S(2)}, u32[]{:S(2)}) async-start(bf16[6,192,180,2,45]{1,3,4,0,2:T(2,128)(2,1)} %copy.168), calls=%async_computation.4 | async-start | bytes 99532800 | tf_op jit(solution)/shard_map/all_to_all | solution.py:88
where the time goes:
time: 6850 us; the launch traced here: 6790 us
  local copies, waits for them, and re-layouts  2960 us (43%)
  waiting for transfers between devices  1530 us (22%)
  blocking collectives  1240 us (18%)
  other arithmetic  637 us (9%)
  matrix products  234 us (3%)
  loops' own time  131 us (2%)
    mul x6, local copies, waits for them, and re-layouts, local_layer(): jax.nn.gelu(grid_out.astype(jnp.float32), approximate=False)  832 us
    all_to_all x1, blocking collectives, local_layer(): grid_out = lax.all_to_all(grid_out, 'lon', 3, 1, tiled=True)  620 us
    all_to_all x1, blocking collectives, local_layer(): mixed_coef = lax.all_to_all(mixed_coef, 'lon', 1, 2, tiled=True)  620 us
    all_to_all x1, waiting for transfers between devices, local_layer(): lax.all_to_all(grid_field.astype(jnp.bfloat16), 'lon', 1, 3, tiled=True)  606 us
    all_to_all x1, waiting for transfers between devices, local_layer(): spec_grid = lax.all_to_all(spec_grid, 'lat', 2, 4, tiled=True)  535 us
    reshape x2, local copies, waits for them, and re-layouts, local_layer(): fourier.astype(jnp.bfloat16)  464 us
    all_to_all x1, waiting for transfers between devices, local_layer(): spec_coef = lax.all_to_all(spec_coef, 'lon', 2, 1, tiled=True)  387 us
    all_to_all x1, local copies, waits for them, and re-layouts, local_layer(): mixed_coef = lax.all_to_all(mixed_coef, 'lon', 1, 2, tiled=True)  174 us
  transfers between devices with their start and end apart: 4, of which 3 were waited for; matrix products, arithmetic and copies ran while one was open for 8% of the time, Pallas kernels for 0%

commit v1 on v0

v1 whole, which is shorter than its diff:
```python
import functools
import math
import numpy as np
import jax
import jax.numpy as jnp
from jax import lax
from jax.experimental import pallas as pl
from jax.experimental.pallas import tpu as pltpu
from jax.sharding import PartitionSpec as P

BF = jnp.bfloat16
F32 = jnp.float32
LANE = 128


def legendre_table(n_lat, n_deg):
    colat = (np.arange(n_lat) + 0.5) * (math.pi / n_lat)
    cos_t = np.cos(colat)[None, :]
    m_int = np.arange(n_deg)[:, None]
    m_col = m_int.astype(np.float64)
    deg = np.arange(1, n_deg + 1).astype(np.float64)
    cum_log = np.concatenate([np.zeros(1), np.cumsum(0.5 * np.log((2 * deg + 1) / (2 * deg)))])
    log_diag = 0.5 * math.log(0.5) + cum_log[m_int] + m_col * np.log(np.sin(colat))[None, :]
    one = np.zeros((n_deg, n_lat))
    two = np.zeros((n_deg, n_lat))
    scale = np.zeros((n_deg, n_lat))
    table = np.zeros((n_deg, n_deg, n_lat))
    for l in range(n_deg):
        start = m_int == l
        above = m_int < l
        coef_a = np.sqrt((4.0 * l * l - 1.0) / np.maximum(l * l - m_col * m_col, 1.0)) if l else np.ones_like(m_col)
        coef_b = np.sqrt(np.maximum((l - 1.0) ** 2 - m_col * m_col, 0.0) / max(4.0 * (l - 1.0) ** 2 - 1.0, 1.0))
        value = coef_a * (cos_t * one - coef_b * two)
        renorm = np.maximum(np.abs(value), 1.0)
        new_one = np.where(start, 1.0, np.where(above, value / renorm, 0.0))
        two = np.where(above, one / renorm, 0.0)
        scale = np.where(start, log_diag, np.where(above, scale + np.log(renorm), 0.0))
        one = new_one
        table[l] = np.where(start | above, one * np.exp(scale), 0.0)
    return table


def fejer_weights(n_lat):
    colat = (np.arange(n_lat) + 0.5) * (math.pi / n_lat)
    n = np.arange(1, n_lat // 2 + 1).astype(np.float64)
    series = np.cos(2.0 * colat[:, None] * n[None, :]) / (4.0 * n * n - 1.0)
    return (2.0 / n_lat) * (1.0 - 2.0 * series.sum(axis=1))


def build_tables(n_lat, n_lon, n_deg, lat_devs, lon_devs, row_pad):
    rows = n_lat // lat_devs
    cols = n_lon // lon_devs
    m_per = n_deg // lat_devs
    leg = legendre_table(n_lat, n_deg)
    leg_w = leg * (fejer_weights(n_lat) / n_lon)[None, None, :]
    angle = (2.0 * math.pi / n_lon) * ((np.arange(n_deg)[:, None] * np.arange(n_lon)[None, :]) % n_lon)
    weight = np.where(np.arange(n_deg) == 0, 1.0, 2.0)[:, None]
    fwd = np.stack([np.cos(angle), -np.sin(angle)], axis=1)
    inv = np.stack([weight * np.cos(angle), -weight * np.sin(angle)], axis=1)
    t_fwd = np.zeros((lat_devs, lon_devs, lon_devs, 2 * n_deg, cols))
    t_inv = np.zeros((lat_devs, lon_devs, lon_devs, cols, 2 * n_deg))
    p_fwd = np.zeros((lat_devs, m_per, n_deg, lat_devs, row_pad))
    p_inv = np.zeros((lat_devs, m_per, lat_devs, row_pad, n_deg))
    for d in range(lat_devs):
        order = np.concatenate([(d ^ t) + lat_devs * np.arange(m_per) for t in range(lat_devs)])
        for h in range(lon_devs):
            for s in range(lon_devs):
                cut = slice((h ^ s) * cols, ((h ^ s) + 1) * cols)
                t_fwd[d, h, s] = fwd[order].reshape(2 * n_deg, n_lon)[:, cut]
                t_inv[d, h, s] = inv[order].reshape(2 * n_deg, n_lon)[:, cut].T
        mine = d + lat_devs * np.arange(m_per)
        for t in range(lat_devs):
            cut = slice((d ^ t) * rows, ((d ^ t) + 1) * rows)
            p_fwd[d, :, :, t, :rows] = leg_w[:, mine, cut].transpose(1, 0, 2)
            p_inv[d, :, t, :rows, :] = leg[:, mine, cut].transpose(1, 2, 0)
    p_fwd = p_fwd.reshape(lat_devs, m_per, n_deg, lat_devs * row_pad)
    p_inv = p_inv.reshape(lat_devs, m_per, lat_devs * row_pad, n_deg)
    return [np.asarray(np.asarray(x, np.float32), dtype=BF) for x in (t_fwd, t_inv, p_fwd, p_inv)]


def dot(a, b):
    return jnp.dot(a, b, preferred_element_type=F32)


def fourier_kernel(sp, f_ref, r_ref, t_ref, o0, o1, o2, o3, scr):
    outs = (o0, o1, o2, o3)
    k_n = r_ref.shape[0]
    m2 = t_ref.shape[3]
    per, row_pad = o0.shape[0], o0.shape[1]
    scr[pl.ds(k_n * m2, (row_pad - k_n) * m2), :] = jnp.zeros(((row_pad - k_n) * m2, LANE), F32)

    def step(p, _):
        k = jnp.minimum(2 * p, k_n - 2)
        mine = jnp.concatenate([f_ref[0, k], f_ref[0, k + 1]], axis=1).astype(BF)
        other = jnp.concatenate([r_ref[k], r_ref[k + 1]], axis=1)
        acc = dot(t_ref[0, 0, 0], mine) + dot(t_ref[0, 0, 1], other)
        base = pl.multiple_of(k * m2, 8)
        scr[pl.ds(base, m2), :] = acc[:, :LANE]
        scr[pl.ds(base + m2, m2), :] = acc[:, LANE:]
        return 0

    lax.fori_loop(0, (k_n + 1) // 2, step, 0)

    def spread(i, _):
        for t in range(4):
            outs[t][i] = scr[pl.ds(t * per + i, row_pad, stride=m2), :].astype(BF)
        return 0

    lax.fori_loop(0, per, spread, 0)


def analysis_kernel(sp, x0, x1, x2, x3, p_ref, o_ref, scr, *, stride):
    xs = (x0, x1, x2, x3)
    m_per, n_deg = p_ref.shape[1], p_ref.shape[2]
    m_pad = o_ref.shape[2]
    for r in range(2):
        scr[r, pl.ds(m_per * stride, (m_pad - m_per) * stride), :] = jnp.zeros(((m_pad - m_per) * stride, LANE), F32)

    def step(i, _):
        re = jnp.concatenate([x[2 * i] for x in xs], axis=0)
        im = jnp.concatenate([x[2 * i + 1] for x in xs], axis=0)
        acc = dot(p_ref[0, i], jnp.concatenate([re, im], axis=1))
        base = pl.multiple_of(i * stride, 8)
        scr[0, pl.ds(base, n_deg), :] = acc[:, :LANE]
        scr[1, pl.ds(base, n_deg), :] = acc[:, LANE:]
        return 0

    lax.fori_loop(0, m_per, step, 0)

    def spread(l, _):
        for r in range(2):
            o_ref[r, l] = scr[r, pl.ds(l, m_pad, stride=stride), :].astype(BF)
        return 0

    lax.fori_loop(0, n_deg, spread, 0)


def mixing_kernel(*refs, parts):
    a_refs, w_ref, o_refs = refs[:parts], refs[parts], refs[parts + 1:]
    cw = o_refs[0].shape[3]
    m_pad = o_refs[0].shape[2]

    def step(l, _):
        re = jnp.concatenate([a[0, l] for a in a_refs], axis=1)
        im = jnp.concatenate([a[1, l] for a in a_refs], axis=1)
        lhs = jnp.concatenate([jnp.concatenate([re, -im], axis=1), jnp.concatenate([im, re], axis=1)], axis=0)
        acc = dot(lhs, w_ref[l]).astype(BF)
        for j, o in enumerate(o_refs):
            o[0, l] = acc[:m_pad, j * cw:(j + 1) * cw]
            o[1, l] = acc[m_pad:, j * cw:(j + 1) * cw]
        return 0

    lax.fori_loop(0, w_ref.shape[0], step, 0)


def synthesis_kernel(sp, b_ref, p_ref, o0, o1, o2, o3, scr, *, stride):
    outs = (o0, o1, o2, o3)
    m_per, n_deg = p_ref.shape[1], p_ref.shape[3]
    m_pad = b_ref.shape[2]
    row_pad = o0.shape[1]

    def load(l, _):
        base = pl.multiple_of(l * stride, 8)
        for r in range(2):
            scr[r, pl.ds(base, m_pad), :] = b_ref[r, l].astype(F32)
        return 0

    lax.fori_loop(0, n_deg, load, 0)

    def step(i, _):
        x = jnp.concatenate([scr[r, pl.ds(i, n_deg, stride=stride), :] for r in range(2)], axis=1).astype(BF)
        acc = dot(p_ref[0, i], x).astype(BF)
        for t in range(4):
            outs[t][2 * i] = acc[t * row_pad:(t + 1) * row_pad, :LANE]
            outs[t][2 * i + 1] = acc[t * row_pad:(t + 1) * row_pad, LANE:]
        return 0

    lax.fori_loop(0, m_per, step, 0)


def inverse_kernel(sp, x0, x1, x2, x3, t_ref, own_ref, snd_ref, scr, *, stride):
    xs = (x0, x1, x2, x3)
    per, row_pad = x0.shape[0], x0.shape[1]
    k_n = own_ref.shape[0]

    def load(i, _):
        for t in range(4):
            base = pl.multiple_of((t * per + i) * stride, 8)
            scr[pl.ds(base, row_pad), :] = xs[t][i].astype(F32)
        return 0

    lax.fori_loop(0, per, load, 0)

    def step(p, _):
        k = jnp.minimum(2 * p, k_n - 2)
        x = jnp.concatenate([scr[pl.ds(k + e, 4 * per, stride=stride), :] for e in range(2)], axis=1).astype(BF)
        own = dot(t_ref[0, 0, 0], x).astype(BF)
        own_ref[k] = own[:, :LANE]
        own_ref[k + 1] = own[:, LANE:]
        snd = dot(t_ref[0, 0, 1], x).astype(BF)
        snd_ref[k] = snd[:, :LANE]
        snd_ref[k + 1] = snd[:, LANE:]
        return 0

    lax.fori_loop(0, (k_n + 1) // 2, step, 0)


def final_kernel(sp, f_ref, y_ref, *rest):
    out_ref = rest[-1]
    y = y_ref[...].astype(F32)
    out_ref[0] = f_ref[0] + 0.5 * y * (1.0 + lax.erf(y * (2.0 ** -0.5)))


def solution(mesh):
    lat_devs = mesh.shape['lat']
    lon_devs = mesh.shape['lon']

    def local_layer(grid_field, mix_weight):
        batch, chans, rows, cols = grid_field.shape
        n_lat, n_lon = rows * lat_devs, cols * lon_devs
        n_deg = mix_weight.shape[0]
        m_per = n_deg // lat_devs
        per = 2 * m_per
        pad = -(-rows // 16) * 16
        fields = batch // lon_devs
        cw = chans
        parts = chans // cw
        t_fwd, t_inv, p_fwd, p_inv = (jnp.asarray(x) for x in build_tables(n_lat, n_lon, n_deg, lat_devs, lon_devs, pad))
        lat = lax.axis_index('lat').astype(jnp.int32)
        lon = lax.axis_index('lon').astype(jnp.int32)
        field = grid_field.transpose(0, 2, 3, 1)
        weight = mix_weight.transpose(0, 3, 1, 2).reshape(n_deg, 2 * chans, chans)
        swap = [(0, 1), (1, 0)]
        vmem = pltpu.CompilerParams(vmem_limit_bytes=60 * 2 ** 20)

        def call(kernel, sp, grid, ins, outs, scratch, args, cost, aliases={}):
            return pl.pallas_call(
                kernel,
                grid_spec=pltpu.PrefetchScalarGridSpec(num_scalar_prefetch=1, grid=grid, in_specs=ins, out_specs=outs[1], scratch_shapes=scratch),
                out_shape=outs[0], compiler_params=vmem, input_output_aliases=aliases,
                cost_estimate=pl.CostEstimate(flops=cost, bytes_accessed=0, transcendentals=0))(sp, *args)

        spec_x = pl.BlockSpec((per, pad, LANE), lambda c, sp: (0, 0, c))
        shape_x = jax.ShapeDtypeStruct((per, pad, cw), BF)
        shape_y = jax.ShapeDtypeStruct((rows, cols, cw), BF)
        spec_y = pl.BlockSpec((rows, cols, LANE), lambda c, sp: (0, 0, c))
        spec_s = pl.BlockSpec((2, n_deg, pad, LANE), lambda c, sp: (0, 0, 0, c))
        shape_s = jax.ShapeDtypeStruct((2, n_deg, pad, cw), BF)
        spec_t = lambda a, b: pl.BlockSpec((1, 1, lon_devs, a, b), lambda c, sp: (sp[1], sp[2], 0, 0, 0))
        spec_p = lambda a, b: pl.BlockSpec((1, m_per, a, b), lambda c, sp: (sp[1], 0, 0, 0))
        n_blk = cw // LANE
        unit = int(1e9)

        def lat_swap(xs):
            return [xs[0]] + [lax.ppermute(xs[t], 'lat', [(s, s ^ t) for s in range(lat_devs)]) for t in range(1, lat_devs)]

        out = None
        spectral = []
        sps = [jnp.stack([lon * fields + q, lat, lon, (1 - lon) * fields + q]) for q in range(fields)]
        received = []
        for q in range(fields):
            send = lax.dynamic_index_in_dim(field, (1 - lon) * fields + q, 0, keepdims=False).astype(BF)
            received.append(lax.ppermute(send, 'lon', swap))
        for q in range(fields):
            sp = sps[q]
            xs = call(fourier_kernel, sp, (n_blk,),
                      [pl.BlockSpec((1, rows, cols, LANE), lambda c, sp: (sp[0], 0, 0, c)), spec_y, spec_t(2 * n_deg, cols)],
                      ([shape_x] * 4, [spec_x] * 4), [pltpu.VMEM((pad * 2 * n_deg, LANE), F32)],
                      (field, received[q], t_fwd), 20 * unit)
            xs = lat_swap(xs)
            st = -(-n_deg // 8) * 8
            spectral.append(call(functools.partial(analysis_kernel, stride=st), sp, (n_blk,),
                                 [spec_x] * 4 + [spec_p(n_deg, lat_devs * pad)],
                                 (shape_s, spec_s), [pltpu.VMEM((2, pad * st, LANE), F32)],
                                 (*xs, p_fwd), 20 * unit))
        blk = 6
        own_y, got_y = [], []
        for q in range(fields):
            sp = sps[q]
            mixed = pl.pallas_call(
                functools.partial(mixing_kernel, parts=parts), grid=(n_deg // blk,),
                in_specs=[pl.BlockSpec((2, blk, pad, cw), lambda l: (0, l, 0, 0))] * parts + [pl.BlockSpec((blk, 2 * chans, chans), lambda l: (l, 0, 0))],
                out_specs=[pl.BlockSpec((2, blk, pad, cw), lambda l: (0, l, 0, 0))] * parts,
                out_shape=[shape_s] * parts, compiler_params=vmem,
                cost_estimate=pl.CostEstimate(flops=40 * unit, bytes_accessed=0, transcendentals=0))(spectral[q], weight)
            xs = call(functools.partial(synthesis_kernel, stride=56), sp, (n_blk,),
                      [spec_s, spec_p(lat_devs * pad, n_deg)], ([shape_x] * 4, [spec_x] * 4),
                      [pltpu.VMEM((2, n_deg * 56, LANE), F32)], (mixed[0], p_inv), 20 * unit)
            xs = lat_swap(xs)
            own, snd = call(functools.partial(inverse_kernel, stride=56), sp, (n_blk,),
                            [spec_x] * 4 + [spec_t(cols, 2 * n_deg)], ([shape_y] * 2, [spec_y] * 2),
                            [pltpu.VMEM((4 * per * 56, LANE), F32)], (*xs, t_inv), 20 * unit)
            own_y.append(own)
            got_y.append(lax.ppermute(snd, 'lon', swap))
        kb = 9
        out_shape = jax.ShapeDtypeStruct(field.shape, F32)

        def finish(out, y, q, which):
            fspec = pl.BlockSpec((1, kb, cols, LANE), lambda k, c, sp: (sp[which], k, 0, c))
            ins = [fspec, pl.BlockSpec((kb, cols, LANE), lambda k, c, sp: (k, 0, c))]
            args = [field, y]
            aliases = {}
            if out is not None:
                ins.append(pl.BlockSpec(memory_space=pl.ANY))
                args.append(out)
                aliases = {3: 0}
            return call(final_kernel, sps[q], (rows // kb, n_blk), ins, (out_shape, fspec), [], args, 8 * unit, aliases)

        for q in range(fields):
            out = finish(out, own_y[q], q, 0)
        for q in range(fields):
            out = finish(out, got_y[q], q, 3)
        return out.transpose(0, 3, 1, 2)

    field_spec = P('member', None, 'lat', 'lon')
    return jax.shard_map(local_layer, mesh=mesh, in_specs=(field_spec, P()), out_specs=field_spec, check_vma=False)
```

time: 6850 us -> 1400 us (0.20)
  local copies, waits for them, and re-layouts: 2960 us -> 89.3 us
  blocking collectives: 1240 us -> 0 us
  waiting for transfers between devices: 1530 us -> 590 us
  Pallas kernels: 0 us -> 696 us
  other arithmetic: 637 us -> 1.9 us
  matrix products: 234 us -> 0 us
  loops' own time: 131 us -> 0 us
    all_to_all x4 -> x0, waiting for transfers between devices: 1530 us -> none  [the longest x1 606 us: local_layer(): lax.all_to_all(grid_field.astype(jnp.bfloat16), 'lon', 1, 3, tiled=True)]
    all_to_all x2 -> x0, blocking collectives: 1240 us -> none  [the longest x1 620 us: local_layer(): grid_out = lax.all_to_all(grid_out, 'lon', 3, 1, tiled=True)]
    reshape x7 -> x0, local copies, waits for them, and re-layouts: 857 us -> none  [the longest x2 464 us: local_layer(): fourier.astype(jnp.bfloat16)]
    mul x6 -> x0, local copies, waits for them, and re-layouts: 832 us -> none  [local_layer(): jax.nn.gelu(grid_out.astype(jnp.float32), approximate=False)]
    all_to_all x7 -> x0, local copies, waits for them, and re-layouts: 705 us -> none  [the longest x1 174 us: local_layer(): mixed_coef = lax.all_to_all(mixed_coef, 'lon', 1, 2, tiled=True)]
    pallas_call x0 -> x21, Pallas kernels: none -> 696 us  [the longest x18 510 us: call(): pl.pallas_call(kernel, grid_spec=pltpu.PrefetchScalarGridSpec(num_scalar_...]
    ppermute x0 -> x24, waiting for transfers between devices: none -> 590 us  [the longest x3 275 us: local_layer(): received.append(lax.ppermute(send, 'lon', swap))]
    convert_element_type x5 -> x1, local copies, waits for them, and re-layouts: 362 us -> 19.6 us  [local_layer(): lax.dynamic_index_in_dim(field, (1 - lon) * fields + q, 0, keepdims=False)]
  transfers between devices with their start and end apart: 4 -> 24, of which waited for: 3 -> 9; matrix products, arithmetic and copies ran while one was open for 8% -> 5% of each run, Pallas kernels for 0% -> 48%
where the time goes in v1:
time: 1400 us
  Pallas kernels  696 us (50%)
  waiting for transfers between devices  590 us (42%)
  local copies, waits for them, and re-layouts  89.3 us (6%)
  starting transfers between devices  23.5 us (2%)
    pallas_call x18, Pallas kernels, call(): pl.pallas_call(kernel, grid_spec=pltpu.PrefetchScalarGridSpec(num_scalar_...  510 us
    ppermute x3, waiting for transfers between devices, local_layer(): received.append(lax.ppermute(send, 'lon', swap))  275 us
    ppermute x18, waiting for transfers between devices, lat_swap(): lax.ppermute(xs[t], 'lat', [(s, s ^ t) for s in range(lat_devs)])  235 us
    pallas_call x3, Pallas kernels, local_layer(): pl.pallas_call(functools.partial(mixing_kernel, parts=parts), grid=(n_deg...  186 us
    ppermute x3, waiting for transfers between devices, local_layer(): got_y.append(lax.ppermute(snd, 'lon', swap))  79.4 us
    transpose x1, local copies, waits for them, and re-layouts, local_layer(): weight = mix_weight.transpose(0, 3, 1, 2).reshape(n_deg, 2 * chans, chans)  69.7 us
  transfers between devices with their start and end apart: 24, of which 9 were waited for; matrix products, arithmetic and copies ran while one was open for 5% of the time, Pallas kernels for 48%

profile of v1, /device:TPU:0, one launch (start us, length us, event | category | flops | bytes accessed | tf_op | source)
XLA Modules:
  0.0 1400.9 jit_solution(14924419892965466598)
XLA Ops:
  0.0 19.6 %fusion.2 = (bf16[45,180,384]{2,1,0:T(8,128)(2,1)}, bf16[45,180,384]{2,1,0:T(8,128)(2,1)}, bf16[45,180,384]{2,1,0:T(8,128)(2,1)}) fusion(f32[6,384,45,180]{1,3,2,0:T(8,128)} %param.6, s32[]{:T(128)S(6)} %select_n.12, s32[]{:T(128)S(6)} %select_n.10, s32[]{:T(128)S(6)} %select_n.11), kind=kLoop, calls=%fused_computation.5 | loop fusion | bytes 37324812 | tf_op jit(solution)/shard_map/convert_element_type | solution.py:262
  19.6 3.3 collective-permute-start.16
  22.9 2.0 collective-permute-start
  24.9 69.7 %copy.12 = bf16[180,2,384,384]{3,2,1,0:T(8,128)(2,1)} copy(bf16[180,2,384,384]{3,1,2,0:T(2,128)(2,1)} %bitcast.7) | data formatting | bytes 212336640 | tf_op jit(solution)/shard_map/transpose | solution.py:232
  94.6 0.7 pad_add_fusion.sp
  95.2 0.6 pad_add_fusion.1.sp
  95.8 0.6 pad_add_fusion.2.sp
  96.5 64.2 %collective-permute-done.16.r_ref = bf16[45,180,384]{2,1,0:T(8,128)(2,1)} collective-permute-done((bf16[45,180,384]{2,1,0:T(8,128)(2,1)}, bf16[45,180,384]{2,1,0:T(8,128)(2,1)}, u32[]{:S(2)}, u32[]{:S(2)}) %collective-permute-start.16) | collective-permute-done | bytes 6220832 | tf_op jit(solution)/shard_map/ppermute | solution.py:263
  160.7 29.3 %shard_map.74 = (bf16[90,48,384]{2,1,0:T(8,128)(2,1)}, bf16[90,48,384]{2,1,0:T(8,128)(2,1)}, bf16[90,48,384]{2,1,0:T(8,128)(2,1)}, bf16[90,48,384]{2,1,0:T(8,128)(2,1)}) custom-call(s32[4]{0:T(128)} %pad_add_fusion.2.sp, f32[6,45,180,384]{3,2,1,0:T(8,128)} %bitcast.4.f_ref, bf16[45,180,384]{2,1,0:T(8,128)(2,1)} %collective-permute-done.16.r_ref, ...), custom_call_target="tpu_custom_call" | custom-call | flops 20000000000 | tf_op jit(solution)/shard_map/pallas_call | solution.py:237
  190.0 2.1 collective-permute-start.18
  192.2 104.8 %collective-permute-done.8.r_ref = bf16[45,180,384]{2,1,0:T(8,128)(2,1)} collective-permute-done((bf16[45,180,384]{2,1,0:T(8,128)(2,1)}, bf16[45,180,384]{2,1,0:T(8,128)(2,1)}, u32[]{:S(2)}, u32[]{:S(2)}) %collective-permute-start.8) | collective-permute-done | bytes 6220832 | tf_op jit(solution)/shard_map/ppermute | solution.py:263
  296.9 29.2 %shard_map.69 = (bf16[90,48,384]{2,1,0:T(8,128)(2,1)}, bf16[90,48,384]{2,1,0:T(8,128)(2,1)}, bf16[90,48,384]{2,1,0:T(8,128)(2,1)}, bf16[90,48,384]{2,1,0:T(8,128)(2,1)}) custom-call(s32[4]{0:T(128)} %pad_add_fusion.1.sp, f32[6,45,180,384]{3,2,1,0:T(8,128)} %bitcast.4.f_ref, bf16[45,180,384]{2,1,0:T(8,128)(2,1)} %collective-permute-done.8.r_ref, ...), custom_call_target="tpu_custom_call" | custom-call | flops 20000000000 | tf_op jit(solution)/shard_map/pallas_call | solution.py:237
  326.1 106.3 %collective-permute-done.r_ref = bf16[45,180,384]{2,1,0:T(8,128)(2,1)} collective-permute-done((bf16[45,180,384]{2,1,0:T(8,128)(2,1)}, bf16[45,180,384]{2,1,0:T(8,128)(2,1)}, u32[]{:S(2)}, u32[]{:S(2)}) %collective-permute-start) | collective-permute-done | bytes 6220832 | tf_op jit(solution)/shard_map/ppermute | solution.py:263
  432.4 1.8 collective-permute-start.10
  434.2 29.2 %shard_map.64 = (bf16[90,48,384]{2,1,0:T(8,128)(2,1)}, bf16[90,48,384]{2,1,0:T(8,128)(2,1)}, bf16[90,48,384]{2,1,0:T(8,128)(2,1)}, bf16[90,48,384]{2,1,0:T(8,128)(2,1)}) custom-call(s32[4]{0:T(128)} %pad_add_fusion.sp, f32[6,45,180,384]{3,2,1,0:T(8,128)} %bitcast.4.f_ref, bf16[45,180,384]{2,1,0:T(8,128)(2,1)} %collective-permute-done.r_ref, ...), custom_call_target="tpu_custom_call" | custom-call | flops 20000000000 | tf_op jit(solution)/shard_map/pallas_call | solution.py:237
  463.9 1.7 collective-permute-start.2
  465.6 40.2 %shard_map.75.refs_0_ = bf16[2,180,48,384]{3,2,1,0:T(8,128)(2,1)} custom-call(s32[4]{0:T(128)} %pad_add_fusion.2.sp, bf16[90,48,384]{2,1,0:T(8,128)(2,1)} %get-tuple-element.53.x0, bf16[90,48,384]{2,1,0:T(8,128)(2,1)} %collective-permute-done.17.x1, bf16[90,48,384]{2,1,0:T(8,128)(2,1)} %collective-permute-done.18.x2, ...), custom_call_target="tpu_custom_call" | custom-call | flops 20000000000 | tf_op jit(solution)/shard_map/pallas_call | solution.py:237
  505.8 62.1 %shard_map.76.b_ref = bf16[2,180,48,384]{3,2,1,0:T(8,128)(2,1)} custom-call(bf16[2,180,48,384]{3,2,1,0:T(8,128)(2,1)} %shard_map.75.refs_0_, bf16[180,768,384]{2,1,0:T(8,128)(2,1)} %bitcast.8.refs_1_), custom_call_target="tpu_custom_call" | custom-call | flops 40000000000 | tf_op jit(solution)/shard_map/pallas_call | solution.py:280
  567.8 9.6 collective-permute-done.11.x3
  577.4 40.2 %shard_map.70.refs_0_ = bf16[2,180,48,384]{3,2,1,0:T(8,128)(2,1)} custom-call(s32[4]{0:T(128)} %pad_add_fusion.1.sp, bf16[90,48,384]{2,1,0:T(8,128)(2,1)} %get-tuple-element.44.x0, bf16[90,48,384]{2,1,0:T(8,128)(2,1)} %collective-permute-done.9.x1, bf16[90,48,384]{2,1,0:T(8,128)(2,1)} %collective-permute-done.10.x2, ...), custom_call_target="tpu_custom_call" | custom-call | flops 20000000000 | tf_op jit(solution)/shard_map/pallas_call | solution.py:237
  617.7 62.0 %shard_map.71.b_ref = bf16[2,180,48,384]{3,2,1,0:T(8,128)(2,1)} custom-call(bf16[2,180,48,384]{3,2,1,0:T(8,128)(2,1)} %shard_map.70.refs_0_, bf16[180,768,384]{2,1,0:T(8,128)(2,1)} %bitcast.8.refs_1_), custom_call_target="tpu_custom_call" | custom-call | flops 40000000000 | tf_op jit(solution)/shard_map/pallas_call | solution.py:280
  679.7 37.5 %shard_map.77 = (bf16[90,48,384]{2,1,0:T(8,128)(2,1)}, bf16[90,48,384]{2,1,0:T(8,128)(2,1)}, bf16[90,48,384]{2,1,0:T(8,128)(2,1)}, bf16[90,48,384]{2,1,0:T(8,128)(2,1)}) custom-call(s32[4]{0:T(128)} %pad_add_fusion.2.sp, bf16[2,180,48,384]{3,2,1,0:T(8,128)(2,1)} %shard_map.76.b_ref, bf16[4,45,192,180]{3,2,1,0:T(8,128)(2,1)} %constant.40.clone.p_ref), custom_call_target="tpu_custom_call" | custom-call | flops 20000000000 | tf_op jit(solution)/shard_map/pallas_call | solution.py:237
  717.1 0.5 collective-permute-start.20
  717.6 37.5 %shard_map.72 = (bf16[90,48,384]{2,1,0:T(8,128)(2,1)}, bf16[90,48,384]{2,1,0:T(8,128)(2,1)}, bf16[90,48,384]{2,1,0:T(8,128)(2,1)}, bf16[90,48,384]{2,1,0:T(8,128)(2,1)}) custom-call(s32[4]{0:T(128)} %pad_add_fusion.1.sp, bf16[2,180,48,384]{3,2,1,0:T(8,128)(2,1)} %shard_map.71.b_ref, bf16[4,45,192,180]{3,2,1,0:T(8,128)(2,1)} %constant.40.clone.p_ref), custom_call_target="tpu_custom_call" | custom-call | flops 20000000000 | tf_op jit(solution)/shard_map/pallas_call | solution.py:237
  755.2 1.8 collective-permute-start.13
  757.1 40.2 %shard_map.65.refs_0_ = bf16[2,180,48,384]{3,2,1,0:T(8,128)(2,1)} custom-call(s32[4]{0:T(128)} %pad_add_fusion.sp, bf16[90,48,384]{2,1,0:T(8,128)(2,1)} %get-tuple-element.35.x0, bf16[90,48,384]{2,1,0:T(8,128)(2,1)} %collective-permute-done.1.x1, bf16[90,48,384]{2,1,0:T(8,128)(2,1)} %collective-permute-done.2.x2, ...), custom_call_target="tpu_custom_call" | custom-call | flops 20000000000 | tf_op jit(solution)/shard_map/pallas_call | solution.py:237
  797.3 62.1 %shard_map.66.b_ref = bf16[2,180,48,384]{3,2,1,0:T(8,128)(2,1)} custom-call(bf16[2,180,48,384]{3,2,1,0:T(8,128)(2,1)} %shard_map.65.refs_0_, bf16[180,768,384]{2,1,0:T(8,128)(2,1)} %bitcast.8.refs_1_), custom_call_target="tpu_custom_call" | custom-call | flops 40000000000 | tf_op jit(solution)/shard_map/pallas_call | solution.py:280
  859.3 1.7 collective-permute-start.21
  861.1 37.9 %shard_map.67 = (bf16[90,48,384]{2,1,0:T(8,128)(2,1)}, bf16[90,48,384]{2,1,0:T(8,128)(2,1)}, bf16[90,48,384]{2,1,0:T(8,128)(2,1)}, bf16[90,48,384]{2,1,0:T(8,128)(2,1)}) custom-call(s32[4]{0:T(128)} %pad_add_fusion.sp, bf16[2,180,48,384]{3,2,1,0:T(8,128)(2,1)} %shard_map.66.b_ref, bf16[4,45,192,180]{3,2,1,0:T(8,128)(2,1)} %constant.40.clone.p_ref), custom_call_target="tpu_custom_call" | custom-call | flops 20000000000 | tf_op jit(solution)/shard_map/pallas_call | solution.py:237
  899.1 1.7 collective-permute-start.5
  900.8 1.4 collective-permute-start.6
  902.2 26.7 %shard_map.73 = (bf16[45,180,384]{2,1,0:T(8,128)(2,1)}, bf16[45,180,384]{2,1,0:T(8,128)(2,1)}) custom-call(s32[4]{0:T(128)} %pad_add_fusion.1.sp, bf16[90,48,384]{2,1,0:T(8,128)(2,1)} %get-tuple-element.48.x0, bf16[90,48,384]{2,1,0:T(8,128)(2,1)} %collective-permute-done.12.x1, bf16[90,48,384]{2,1,0:T(8,128)(2,1)} %collective-permute-done.13.x2, ...), custom_call_target="tpu_custom_call" | custom-call | flops 20000000000 | tf_op jit(solution)/shard_map/pallas_call | solution.py:237
  928.9 43.1 %collective-permute-done.21.x2 = bf16[90,48,384]{2,1,0:T(8,128)(2,1)} collective-permute-done((bf16[90,48,384]{2,1,0:T(8,128)(2,1)}, bf16[90,48,384]{2,1,0:T(8,128)(2,1)}, u32[]{:S(2)}, u32[]{:S(2)}) %collective-permute-start.21) | collective-permute-done | bytes 3317792 | tf_op jit(solution)/shard_map/ppermute | solution.py:255
  972.1 1.7 collective-permute-start.15
  973.8 68.7 %collective-permute-done.22.x3 = bf16[90,48,384]{2,1,0:T(8,128)(2,1)} collective-permute-done((bf16[90,48,384]{2,1,0:T(8,128)(2,1)}, bf16[90,48,384]{2,1,0:T(8,128)(2,1)}, u32[]{:S(2)}, u32[]{:S(2)}) %collective-permute-start.22) | collective-permute-done | bytes 3317792 | tf_op jit(solution)/shard_map/ppermute | solution.py:255
  1042.4 26.7 %shard_map.78 = (bf16[45,180,384]{2,1,0:T(8,128)(2,1)}, bf16[45,180,384]{2,1,0:T(8,128)(2,1)}) custom-call(s32[4]{0:T(128)} %pad_add_fusion.2.sp, bf16[90,48,384]{2,1,0:T(8,128)(2,1)} %get-tuple-element.57.x0, bf16[90,48,384]{2,1,0:T(8,128)(2,1)} %copy-done, bf16[90,48,384]{2,1,0:T(8,128)(2,1)} %collective-permute-done.21.x2, ...), custom_call_target="tpu_custom_call" | custom-call | flops 20000000000 | tf_op jit(solution)/shard_map/pallas_call | solution.py:237
  1069.2 1.5 collective-permute-start.23
  1070.7 43.6 %collective-permute-done.5.x2 = bf16[90,48,384]{2,1,0:T(8,128)(2,1)} collective-permute-done((bf16[90,48,384]{2,1,0:T(8,128)(2,1)}, bf16[90,48,384]{2,1,0:T(8,128)(2,1)}, u32[]{:S(2)}, u32[]{:S(2)}) %collective-permute-start.5) | collective-permute-done | bytes 3317792 | tf_op jit(solution)/shard_map/ppermute | solution.py:255
  1114.3 70.2 %collective-permute-done.6.x3 = bf16[90,48,384]{2,1,0:T(8,128)(2,1)} collective-permute-done((bf16[90,48,384]{2,1,0:T(8,128)(2,1)}, bf16[90,48,384]{2,1,0:T(8,128)(2,1)}, u32[]{:S(2)}, u32[]{:S(2)}) %collective-permute-start.6) | collective-permute-done | bytes 3317792 | tf_op jit(solution)/shard_map/ppermute | solution.py:255
  1184.5 26.9 %shard_map.68 = (bf16[45,180,384]{2,1,0:T(8,128)(2,1)}, bf16[45,180,384]{2,1,0:T(8,128)(2,1)}) custom-call(s32[4]{0:T(128)} %pad_add_fusion.sp, bf16[90,48,384]{2,1,0:T(8,128)(2,1)} %get-tuple-element.39.x0, bf16[90,48,384]{2,1,0:T(8,128)(2,1)} %copy-done.2, bf16[90,48,384]{2,1,0:T(8,128)(2,1)} %collective-permute-done.5.x2, ...), custom_call_target="tpu_custom_call" | custom-call | flops 20000000000 | tf_op jit(solution)/shard_map/pallas_call | solution.py:237
  1211.4 1.6 collective-permute-start.7
  1213.0 18.1 %shard_map.79.rest_0_ = f32[6,45,180,384]{3,2,1,0:T(8,128)} custom-call(s32[4]{0:T(128)} %pad_add_fusion.2.sp, f32[6,45,180,384]{3,2,1,0:T(8,128)} %bitcast.4.f_ref, bf16[45,180,384]{2,1,0:T(8,128)(2,1)} %get-tuple-element.64.y_ref), custom_call_target="tpu_custom_call" | custom-call | flops 8000000000 | tf_op jit(solution)/shard_map/pallas_call | solution.py:237
  1231.1 18.1 %shard_map.80.rest_0_ = f32[6,45,180,384]{3,2,1,0:T(8,128)} custom-call(s32[4]{0:T(128)} %pad_add_fusion.1.sp, f32[6,45,180,384]{3,2,1,0:T(8,128)} %bitcast.4.f_ref, bf16[45,180,384]{2,1,0:T(8,128)(2,1)} %get-tuple-element.63.y_ref, f32[6,45,180,384]{3,2,1,0:T(8,128)} %shard_map.79.rest_0_), custom_call_target="tpu_custom_call", output_to_operand_aliasing={{}: (3, {})} | custom-call | flops 8000000000 | tf_op jit(solution)/shard_map/pallas_call | solution.py:237
  1249.1 18.1 %shard_map.81.rest_0_ = f32[6,45,180,384]{3,2,1,0:T(8,128)} custom-call(s32[4]{0:T(128)} %pad_add_fusion.sp, f32[6,45,180,384]{3,2,1,0:T(8,128)} %bitcast.4.f_ref, bf16[45,180,384]{2,1,0:T(8,128)(2,1)} %get-tuple-element.62.y_ref, f32[6,45,180,384]{3,2,1,0:T(8,128)} %shard_map.80.rest_0_), custom_call_target="tpu_custom_call", output_to_operand_aliasing={{}: (3, {})} | custom-call | flops 8000000000 | tf_op jit(solution)/shard_map/pallas_call | solution.py:237
  1267.2 18.1 %shard_map.82.rest_0_ = f32[6,45,180,384]{3,2,1,0:T(8,128)} custom-call(s32[4]{0:T(128)} %pad_add_fusion.2.sp, f32[6,45,180,384]{3,2,1,0:T(8,128)} %bitcast.4.f_ref, bf16[45,180,384]{2,1,0:T(8,128)(2,1)} %collective-permute-done.23.y_ref, f32[6,45,180,384]{3,2,1,0:T(8,128)} %shard_map.81.rest_0_), custom_call_target="tpu_custom_call", output_to_operand_aliasing={{}: (3, {})} | custom-call | flops 8000000000 | tf_op jit(solution)/shard_map/pallas_call | solution.py:237
  1285.3 18.1 %shard_map.83.rest_0_ = f32[6,45,180,384]{3,2,1,0:T(8,128)} custom-call(s32[4]{0:T(128)} %pad_add_fusion.1.sp, f32[6,45,180,384]{3,2,1,0:T(8,128)} %bitcast.4.f_ref, bf16[45,180,384]{2,1,0:T(8,128)(2,1)} %collective-permute-done.15.y_ref, f32[6,45,180,384]{3,2,1,0:T(8,128)} %shard_map.82.rest_0_), custom_call_target="tpu_custom_call", output_to_operand_aliasing={{}: (3, {})} | custom-call | flops 8000000000 | tf_op jit(solution)/shard_map/pallas_call | solution.py:237
  1303.4 79.4 %collective-permute-done.7.y_ref = bf16[45,180,384]{2,1,0:T(8,128)(2,1)} collective-permute-done((bf16[45,180,384]{2,1,0:T(8,128)(2,1)}, bf16[45,180,384]{2,1,0:T(8,128)(2,1)}, u32[]{:S(2)}, u32[]{:S(2)}) %collective-permute-start.7) | collective-permute-done | bytes 6220832 | tf_op jit(solution)/shard_map/ppermute | solution.py:294
  1382.8 18.1 %shard_map.84 = f32[6,45,180,384]{3,2,1,0:T(8,128)} custom-call(s32[4]{0:T(128)} %pad_add_fusion.sp, f32[6,45,180,384]{3,2,1,0:T(8,128)} %bitcast.4.f_ref, bf16[45,180,384]{2,1,0:T(8,128)(2,1)} %collective-permute-done.7.y_ref, f32[6,45,180,384]{3,2,1,0:T(8,128)} %shard_map.83.rest_0_), custom_call_target="tpu_custom_call", output_to_operand_aliasing={{}: (3, {})} | custom-call | flops 8000000000 | tf_op jit(solution)/shard_map/pallas_call | solution.py:237
  (32 shorter events, 0.9 us)
Async XLA Ops:
  19.6 141.1 %collective-permute-start.16 = (bf16[45,180,384]{2,1,0:T(8,128)(2,1)}, bf16[45,180,384]{2,1,0:T(8,128)(2,1)}, u32[]{:S(2)}, u32[]{:S(2)}) collective-permute-start(bf16[45,180,384]{2,1,0:T(8,128)(2,1)} %get-tuple-element.65), channel_id=1, source_target_pairs={{0,4},{4,0},{1,5},{5,1},{2,6},{6,2},{3,7},{7,3}} | collective-permute-start | bytes 18662408 | tf_op jit(solution)/shard_map/ppermute | solution.py:263
  22.9 274.1 %collective-permute-start.8 = (bf16[45,180,384]{2,1,0:T(8,128)(2,1)}, bf16[45,180,384]{2,1,0:T(8,128)(2,1)}, u32[]{:S(2)}, u32[]{:S(2)}) collective-permute-start(bf16[45,180,384]{2,1,0:T(8,128)(2,1)} %get-tuple-element.67), channel_id=1, source_target_pairs={{0,4},{4,0},{1,5},{5,1},{2,6},{6,2},{3,7},{7,3}} | collective-permute-start | bytes 18662408 | tf_op jit(solution)/shard_map/ppermute | solution.py:263
  22.9 409.5 %collective-permute-start = (bf16[45,180,384]{2,1,0:T(8,128)(2,1)}, bf16[45,180,384]{2,1,0:T(8,128)(2,1)}, u32[]{:S(2)}, u32[]{:S(2)}) collective-permute-start(bf16[45,180,384]{2,1,0:T(8,128)(2,1)} %get-tuple-element.66), channel_id=1, source_target_pairs={{0,4},{4,0},{1,5},{5,1},{2,6},{6,2},{3,7},{7,3}} | collective-permute-start | bytes 18662408 | tf_op jit(solution)/shard_map/ppermute | solution.py:263
  190.0 273.4 %collective-permute-start.17 = (bf16[90,48,384]{2,1,0:T(8,128)(2,1)}, bf16[90,48,384]{2,1,0:T(8,128)(2,1)}, u32[]{:S(2)}, u32[]{:S(2)}) collective-permute-start(bf16[90,48,384]{2,1,0:T(8,128)(2,1)} %get-tuple-element.54), channel_id=1, source_target_pairs={{0,1},{1,0},{2,3},{3,2},{4,5},{5,4},{6,7},{7,6}} | collective-permute-start | bytes 9953288 | tf_op jit(solution)/shard_map/ppermute | solution.py:255
  190.0 273.5 %collective-permute-start.18 = (bf16[90,48,384]{2,1,0:T(8,128)(2,1)}, bf16[90,48,384]{2,1,0:T(8,128)(2,1)}, u32[]{:S(2)}, u32[]{:S(2)}) collective-permute-start(bf16[90,48,384]{2,1,0:T(8,128)(2,1)} %get-tuple-element.55), channel_id=1, source_target_pairs={{0,2},{1,3},{2,0},{3,1},{4,6},{5,7},{6,4},{7,5}} | collective-permute-start | bytes 9953288 | tf_op jit(solution)/shard_map/ppermute | solution.py:255
  192.1 271.8 %collective-permute-start.19 = (bf16[90,48,384]{2,1,0:T(8,128)(2,1)}, bf16[90,48,384]{2,1,0:T(8,128)(2,1)}, u32[]{:S(2)}, u32[]{:S(2)}) collective-permute-start(bf16[90,48,384]{2,1,0:T(8,128)(2,1)} %get-tuple-element.56), channel_id=1, source_target_pairs={{0,3},{1,2},{2,1},{3,0},{4,7},{5,6},{6,5},{7,4}} | collective-permute-start | bytes 9953288 | tf_op jit(solution)/shard_map/ppermute | solution.py:255
  326.1 241.7 %collective-permute-start.9 = (bf16[90,48,384]{2,1,0:T(8,128)(2,1)}, bf16[90,48,384]{2,1,0:T(8,128)(2,1)}, u32[]{:S(2)}, u32[]{:S(2)}) collective-permute-start(bf16[90,48,384]{2,1,0:T(8,128)(2,1)} %get-tuple-element.45), channel_id=1, source_target_pairs={{0,1},{1,0},{2,3},{3,2},{4,5},{5,4},{6,7},{7,6}} | collective-permute-start | bytes 9953288 | tf_op jit(solution)/shard_map/ppermute | solution.py:255
  432.4 31.0 %copy-start.1 = (bf16[90,48,384]{2,1,0:T(8,128)(2,1)S(1)}, bf16[90,48,384]{2,1,0:T(8,128)(2,1)}, u32[]{:S(2)}) copy-start(bf16[90,48,384]{2,1,0:T(8,128)(2,1)} %get-tuple-element.47) | copy-start | bytes 9953284
  432.4 135.5 %collective-permute-start.10 = (bf16[90,48,384]{2,1,0:T(8,128)(2,1)}, bf16[90,48,384]{2,1,0:T(8,128)(2,1)}, u32[]{:S(2)}, u32[]{:S(2)}) collective-permute-start(bf16[90,48,384]{2,1,0:T(8,128)(2,1)} %get-tuple-element.46), channel_id=1, source_target_pairs={{0,2},{1,3},{2,0},{3,1},{4,6},{5,7},{6,4},{7,5}} | collective-permute-start | bytes 9953288 | tf_op jit(solution)/shard_map/ppermute | solution.py:255
  463.4 114.0 %collective-permute-start.11 = (bf16[90,48,384]{2,1,0:T(8,128)(2,1)S(1)}, bf16[90,48,384]{2,1,0:T(8,128)(2,1)}, u32[]{:S(2)}, u32[]{:S(2)}) collective-permute-start(bf16[90,48,384]{2,1,0:T(8,128)(2,1)S(1)} %copy-done.1), channel_id=1, source_target_pairs={{0,3},{1,2},{2,1},{3,0},{4,7},{5,6},{6,5},{7,4}} | collective-permute-start | bytes 9953288 | tf_op jit(solution)/shard_map/ppermute | solution.py:255
  463.5 291.7 %collective-permute-start.1 = (bf16[90,48,384]{2,1,0:T(8,128)(2,1)}, bf16[90,48,384]{2,1,0:T(8,128)(2,1)}, u32[]{:S(2)}, u32[]{:S(2)}) collective-permute-start(bf16[90,48,384]{2,1,0:T(8,128)(2,1)} %get-tuple-element.36), channel_id=1, source_target_pairs={{0,1},{1,0},{2,3},{3,2},{4,5},{5,4},{6,7},{7,6}} | collective-permute-start | bytes 9953288 | tf_op jit(solution)/shard_map/ppermute | solution.py:255
  463.9 293.1 %collective-permute-start.2 = (bf16[90,48,384]{2,1,0:T(8,128)(2,1)}, bf16[90,48,384]{2,1,0:T(8,128)(2,1)}, u32[]{:S(2)}, u32[]{:S(2)}) collective-permute-start(bf16[90,48,384]{2,1,0:T(8,128)(2,1)} %get-tuple-element.37), channel_id=1, source_target_pairs={{0,2},{1,3},{2,0},{3,1},{4,6},{5,7},{6,4},{7,5}} | collective-permute-start | bytes 9953288 | tf_op jit(solution)/shard_map/ppermute | solution.py:255
  567.8 189.3 %collective-permute-start.3 = (bf16[90,48,384]{2,1,0:T(8,128)(2,1)}, bf16[90,48,384]{2,1,0:T(8,128)(2,1)}, u32[]{:S(2)}, u32[]{:S(2)}) collective-permute-start(bf16[90,48,384]{2,1,0:T(8,128)(2,1)} %get-tuple-element.38), channel_id=1, source_target_pairs={{0,3},{1,2},{2,1},{3,0},{4,7},{5,6},{6,5},{7,4}} | collective-permute-start | bytes 9953288 | tf_op jit(solution)/shard_map/ppermute | solution.py:255
  717.1 143.9 %collective-permute-start.20 = (bf16[90,48,384]{2,1,0:T(8,128)(2,1)}, bf16[90,48,384]{2,1,0:T(8,128)(2,1)S(1)}, u32[]{:S(2)}, u32[]{:S(2)}) collective-permute-start(bf16[90,48,384]{2,1,0:T(8,128)(2,1)} %get-tuple-element.58), channel_id=1, source_target_pairs={{0,1},{1,0},{2,3},{3,2},{4,5},{5,4},{6,7},{7,6}} | collective-permute-start | bytes 9953288 | tf_op jit(solution)/shard_map/ppermute | solution.py:255
  755.1 143.9 %collective-permute-start.12 = (bf16[90,48,384]{2,1,0:T(8,128)(2,1)}, bf16[90,48,384]{2,1,0:T(8,128)(2,1)}, u32[]{:S(2)}, u32[]{:S(2)}) collective-permute-start(bf16[90,48,384]{2,1,0:T(8,128)(2,1)} %get-tuple-element.49), channel_id=1, source_target_pairs={{0,1},{1,0},{2,3},{3,2},{4,5},{5,4},{6,7},{7,6}} | collective-permute-start | bytes 9953288 | tf_op jit(solution)/shard_map/ppermute | solution.py:255
  755.2 143.9 %collective-permute-start.13 = (bf16[90,48,384]{2,1,0:T(8,128)(2,1)}, bf16[90,48,384]{2,1,0:T(8,128)(2,1)}, u32[]{:S(2)}, u32[]{:S(2)}) collective-permute-start(bf16[90,48,384]{2,1,0:T(8,128)(2,1)} %get-tuple-element.50), channel_id=1, source_target_pairs={{0,2},{1,3},{2,0},{3,1},{4,6},{5,7},{6,4},{7,5}} | collective-permute-start | bytes 9953288 | tf_op jit(solution)/shard_map/ppermute | solution.py:255
  757.0 143.8 %collective-permute-start.14 = (bf16[90,48,384]{2,1,0:T(8,128)(2,1)}, bf16[90,48,384]{2,1,0:T(8,128)(2,1)}, u32[]{:S(2)}, u32[]{:S(2)}) collective-permute-start(bf16[90,48,384]{2,1,0:T(8,128)(2,1)} %get-tuple-element.51), channel_id=1, source_target_pairs={{0,3},{1,2},{2,1},{3,0},{4,7},{5,6},{6,5},{7,4}} | collective-permute-start | bytes 9953288 | tf_op jit(solution)/shard_map/ppermute | solution.py:255
  859.3 112.7 %collective-permute-start.21 = (bf16[90,48,384]{2,1,0:T(8,128)(2,1)}, bf16[90,48,384]{2,1,0:T(8,128)(2,1)}, u32[]{:S(2)}, u32[]{:S(2)}) collective-permute-start(bf16[90,48,384]{2,1,0:T(8,128)(2,1)} %get-tuple-element.59), channel_id=1, source_target_pairs={{0,2},{1,3},{2,0},{3,1},{4,6},{5,7},{6,4},{7,5}} | collective-permute-start | bytes 9953288 | tf_op jit(solution)/shard_map/ppermute | solution.py:255
  861.1 38.0 %copy-start = (bf16[90,48,384]{2,1,0:T(8,128)(2,1)}, bf16[90,48,384]{2,1,0:T(8,128)(2,1)S(1)}, u32[]{:S(2)}) copy-start(bf16[90,48,384]{2,1,0:T(8,128)(2,1)S(1)} %collective-permute-done.20.x1) | copy-start | bytes 9953284
  861.1 181.4 %collective-permute-start.22 = (bf16[90,48,384]{2,1,0:T(8,128)(2,1)}, bf16[90,48,384]{2,1,0:T(8,128)(2,1)}, u32[]{:S(2)}, u32[]{:S(2)}) collective-permute-start(bf16[90,48,384]{2,1,0:T(8,128)(2,1)} %get-tuple-element.60), channel_id=1, source_target_pairs={{0,3},{1,2},{2,1},{3,0},{4,7},{5,6},{6,5},{7,4}} | collective-permute-start | bytes 9953288 | tf_op jit(solution)/shard_map/ppermute | solution.py:255
  899.0 171.6 %collective-permute-start.4 = (bf16[90,48,384]{2,1,0:T(8,128)(2,1)}, bf16[90,48,384]{2,1,0:T(8,128)(2,1)S(1)}, u32[]{:S(2)}, u32[]{:S(2)}) collective-permute-start(bf16[90,48,384]{2,1,0:T(8,128)(2,1)} %get-tuple-element.40), channel_id=1, source_target_pairs={{0,1},{1,0},{2,3},{3,2},{4,5},{5,4},{6,7},{7,6}} | collective-permute-start | bytes 9953288 | tf_op jit(solution)/shard_map/ppermute | solution.py:255
  899.1 215.2 %collective-permute-start.5 = (bf16[90,48,384]{2,1,0:T(8,128)(2,1)}, bf16[90,48,384]{2,1,0:T(8,128)(2,1)}, u32[]{:S(2)}, u32[]{:S(2)}) collective-permute-start(bf16[90,48,384]{2,1,0:T(8,128)(2,1)} %get-tuple-element.41), channel_id=1, source_target_pairs={{0,2},{1,3},{2,0},{3,1},{4,6},{5,7},{6,4},{7,5}} | collective-permute-start | bytes 9953288 | tf_op jit(solution)/shard_map/ppermute | solution.py:255
  900.8 283.7 %collective-permute-start.6 = (bf16[90,48,384]{2,1,0:T(8,128)(2,1)}, bf16[90,48,384]{2,1,0:T(8,128)(2,1)}, u32[]{:S(2)}, u32[]{:S(2)}) collective-permute-start(bf16[90,48,384]{2,1,0:T(8,128)(2,1)} %get-tuple-element.42), channel_id=1, source_target_pairs={{0,3},{1,2},{2,1},{3,0},{4,7},{5,6},{6,5},{7,4}} | collective-permute-start | bytes 9953288 | tf_op jit(solution)/shard_map/ppermute | solution.py:255
  972.1 313.3 %collective-permute-start.15 = (bf16[45,180,384]{2,1,0:T(8,128)(2,1)}, bf16[45,180,384]{2,1,0:T(8,128)(2,1)}, u32[]{:S(2)}, u32[]{:S(2)}) collective-permute-start(bf16[45,180,384]{2,1,0:T(8,128)(2,1)} %get-tuple-element.52), channel_id=1, source_target_pairs={{0,4},{4,0},{1,5},{5,1},{2,6},{6,2},{3,7},{7,3}} | collective-permute-start | bytes 18662408 | tf_op jit(solution)/shard_map/ppermute | solution.py:294
  1069.2 198.0 %collective-permute-start.23 = (bf16[45,180,384]{2,1,0:T(8,128)(2,1)}, bf16[45,180,384]{2,1,0:T(8,128)(2,1)}, u32[]{:S(2)}, u32[]{:S(2)}) collective-permute-start(bf16[45,180,384]{2,1,0:T(8,128)(2,1)} %get-tuple-element.61), channel_id=1, source_target_pairs={{0,4},{4,0},{1,5},{5,1},{2,6},{6,2},{3,7},{7,3}} | collective-permute-start | bytes 18662408 | tf_op jit(solution)/shard_map/ppermute | solution.py:294
  1070.7 113.8 %copy-start.2 = (bf16[90,48,384]{2,1,0:T(8,128)(2,1)}, bf16[90,48,384]{2,1,0:T(8,128)(2,1)S(1)}, u32[]{:S(2)}) copy-start(bf16[90,48,384]{2,1,0:T(8,128)(2,1)S(1)} %collective-permute-done.4.x1) | copy-start | bytes 9953284
  1211.4 171.4 %collective-permute-start.7 = (bf16[45,180,384]{2,1,0:T(8,128)(2,1)}, bf16[45,180,384]{2,1,0:T(8,128)(2,1)}, u32[]{:S(2)}, u32[]{:S(2)}) collective-permute-start(bf16[45,180,384]{2,1,0:T(8,128)(2,1)} %get-tuple-element.43), channel_id=1, source_target_pairs={{0,4},{4,0},{1,5},{5,1},{2,6},{6,2},{3,7},{7,3}} | collective-permute-start | bytes 18662408 | tf_op jit(solution)/shard_map/ppermute | solution.py:294
